TPU v7x, 32 devices: a whole 2x2x4 slice. The times are simulated.
32 devices in a mesh: section: 2 (over core), dp: 16 (over z, y, x).
Axes of the slice: x: 2, y: 2, z: 4, core: 2. Of those that a mesh axis runs over, the one named last changes fastest.
Arguments:
- tokens: bfloat16 [2, 16, 80, 1024], P(None, 'dp'), may hold values from -6 to 6
- w_qkv: bfloat16 [2, 1024, 1536], P('section', 'dp'), may hold values from -0.1875 to 0.1875
- w_output: bfloat16 [2, 512, 1024], P('section', None, 'dp'), may hold values from -0.25 to 0.25
- tangent_value: bfloat16 [2, 2, 1024, 512], P('section', None, 'dp'), may hold values from -0.1875 to 0.1875
- tangent_output: bfloat16 [2, 2, 512, 1024], P('section', None, None, 'dp'), may hold values from -0.25 to 0.25
- layer_gain: float32 [2, 1024], P('section'), may hold values from 0.5 to 1.5
- final_gain: float32 [1024], replicated, may hold values from 0.5 to 1.5
- head: bfloat16 [1024, 1000], P(None, 'section'), may hold values from -0.1875 to 0.1875
Outputs:
- mean_logits: float32 [2, 16, 1000], P(None, 'dp', 'section')
- variance: float32 [2, 16, 1000], P(None, 'dp', 'section')
All inputs are finite; a program needn't handle non-finite values.
Results may differ from a plain program's by a relative error of at most 0.018.
Values may be sent and summed in bfloat16 or wider, within the bound.
A program may use at most 64 MiB of HBM per device.

v0:
```python
import jax
import jax.numpy as jnp
from jax import lax
from jax.sharding import PartitionSpec as P

HEADS = 8
HEAD = 64
TANGENTS = 2
HD = 512
epsilon = 1e-06


def passed_along(block, axis, distance):
    devices = range(lax.axis_size(axis))
    route = [(i - distance, i) for i in devices if i - distance in devices]
    return lax.ppermute(block, axis, route)


def spread(shard, axis, root):
    mine = lax.axis_index(axis) == root
    return lax.psum(jnp.where(mine, shard, jnp.zeros_like(shard)), axis)


def contract(spec, left, right):
    return jnp.einsum(spec, left, right, preferred_element_type=jnp.float32)


def norm_jvp(primal, tangents, gains):
    average = jnp.mean(primal, -1, keepdims=True)
    centred = primal - average
    inverse = lax.rsqrt(jnp.mean(centred * centred, -1, keepdims=True) + epsilon)
    dcentred = tangents - jnp.mean(tangents, -1, keepdims=True)
    dinverse = -(inverse**3) * jnp.mean(centred * dcentred, -1, keepdims=True)
    return (centred * inverse * gains, (dcentred * inverse + centred * dinverse) * gains)


def layer_step(state, qkv_weight, out_weight, value_tangent, out_tangent, gains):
    resid = state.astype(jnp.float32)
    normed_zero, normed_rest = norm_jvp(resid[0], resid[1:], gains)
    normed = jnp.concatenate([normed_zero[None], normed_rest]).astype(jnp.bfloat16)
    streams, batch, tokens_here, width = normed.shape
    projected = contract("sbtd,de->sbte", normed, qkv_weight)
    extra_value = contract("btd,kde->kbte", normed[0], value_tangent)
    queries = projected[..., :HD]
    key_rows = projected[..., HD : 2 * HD]
    values = projected[..., 2 * HD :]
    values = jnp.concatenate([values[:1], values[1:] + extra_value])
    shape_heads = (streams, batch, tokens_here, HEADS, HEAD)
    queries = queries.astype(jnp.bfloat16).reshape(shape_heads)
    key_rows = key_rows.astype(jnp.bfloat16).reshape(shape_heads)
    values = values.astype(jnp.bfloat16).reshape(shape_heads)
    factor = HEAD ** (-0.5)
    scores = contract("bqhe,bkhe->bhqk", queries[0], key_rows[0]) * factor
    probs = jax.nn.softmax(scores, -1)
    dscores = (
        contract("sbqhe,bkhe->sbhqk", queries[1:], key_rows[0])
        + contract("bqhe,sbkhe->sbhqk", queries[0], key_rows[1:])
    ) * factor
    dprobs = probs * (dscores - jnp.sum(probs * dscores, -1, keepdims=True))
    probs_low = probs.astype(jnp.bfloat16)
    dprobs_low = dprobs.astype(jnp.bfloat16)
    attended_zero = contract("bhqk,bkhe->bqhe", probs_low, values[0])
    attended_rest = contract("sbhqk,bkhe->sbqhe", dprobs_low, values[0]) + contract(
        "bhqk,sbkhe->sbqhe", probs_low, values[1:]
    )
    attended = jnp.concatenate([attended_zero[None], attended_rest]).astype(jnp.bfloat16)
    attended = attended.reshape(streams, batch, tokens_here, HD)
    output = contract("sbte,ed->sbtd", attended, out_weight)
    extra_out = contract("bte,ked->kbtd", attended[0], out_tangent)
    output = jnp.concatenate([output[:1], output[1:] + extra_out])
    return (resid + output).astype(jnp.bfloat16)


def shards(tokens, w_qkv, w_output, tangent_value, tangent_output, layer_gain, final_gain, head):
    full_qkv, full_output, full_value_tan, full_output_tan = (
        lax.all_gather(w_qkv, "dp", axis=1, tiled=True),
        lax.all_gather(w_output, "dp", axis=2, tiled=True),
        lax.all_gather(tangent_value, "dp", axis=2, tiled=True),
        lax.all_gather(tangent_output, "dp", axis=3, tiled=True),
    )
    section_gain = layer_gain[0]

    def advance_layer(state):
        return layer_step(
            state, full_qkv[0], full_output[0], full_value_tan[0], full_output_tan[0], section_gain
        )

    def blank_layer(state):
        return jnp.zeros_like(state)

    section_index = lax.axis_index("section")
    section_count = lax.axis_size("section")
    micro_count = tokens.shape[0]
    image_tokens = tokens.shape[2]
    model_width = tokens.shape[3]
    flat_tokens = tokens.reshape(micro_count, image_tokens, model_width)
    entering = jnp.concatenate(
        [
            flat_tokens[None],
            jnp.zeros((TANGENTS, micro_count, image_tokens, model_width), jnp.bfloat16),
        ]
    )

    def advance(step, outgoing):
        incoming = passed_along(outgoing, "section", 1)
        source = jnp.where(step == 0, entering, incoming)
        return lax.cond(section_index == step, advance_layer, blank_layer, source)

    finished = lax.fori_loop(0, section_count, advance, jnp.zeros_like(entering))
    collected = finished[:, :, 0, :]
    features = spread(collected, "section", section_count - 1)
    widened = features.astype(jnp.float32)
    final_zero, final_rest = norm_jvp(widened[0], widened[1:], final_gain)
    normed_final = jnp.concatenate([final_zero[None], final_rest]).astype(jnp.bfloat16)
    logits = contract("sbd,dc->sbc", normed_final, head)
    mean_logits = logits[0][:, None, :]
    variance = jnp.sum(logits[1:] * logits[1:], 0)[:, None, :]
    return (mean_logits, variance)


def solution(mesh):
    return jax.shard_map(
        shards,
        mesh=mesh,
        in_specs=(
            P(None, "dp", None, None),
            P("section", "dp", None),
            P("section", None, "dp"),
            P("section", None, "dp", None),
            P("section", None, None, "dp"),
            P("section", None),
            P(),
            P(None, "section"),
        ),
        out_specs=(P(None, "dp", "section"), P(None, "dp", "section")),
        check_vma=False,
    )
```

profile of v0, /device:TPU:0, one launch (start us, length us, event | category | flops | bytes accessed | tf_op | source)
XLA Modules:
  0.0 363.6 jit_solution(397658022795245036)
XLA Ops:
  7.2 0.7 all-gather.9.cloned.1.call-update
  8.0 1.7 copy.64
  9.8 0.7 all-gather.7.cloned.1.call-update
  10.5 0.5 all-gather.5.cloned.1.call-update
  11.0 2.1 concatenate.31
  13.1 55.5 %all-gather.9.cloned.1.call-done = bf16[1,512,1024]{1,2,0:T(8,128)(2,1)} async-done(((bf16[1,512,64]{1,2,0:T(8,128)(2,1)}), bf16[1,512,1024]{1,2,0:T(8,128)(2,1)}) %all-gather.9.cloned.1.call-update) | async-done | bytes 1048592 | tf_op jit(solution)/shard_map/all_gather | solution.py:77
  68.6 2.3 copy.65
  70.9 59.7 %all-gather.11.cloned.1.call-done = bf16[1,2,512,1024]{2,1,0,3:T(2,128)(2,1)} async-done(((bf16[1,2,512,64]{2,1,0,3:T(2,128)(2,1)}), bf16[1,2,512,1024]{2,1,0,3:T(2,128)(2,1)}) %all-gather.11.cloned.1.call-update) | async-done | bytes 2097168 | tf_op jit(solution)/shard_map/all_gather | solution.py:79
  130.6 6.2 %copy.66 = bf16[1,2,512,1024]{3,2,1,0:T(8,128)(2,1)} copy(bf16[1,2,512,1024]{2,1,0,3:T(2,128)(2,1)} %all-gather.11.cloned.1.call-done) | data formatting | bytes 4194304 | tf_op jit(solution)/shard_map/while | solution.py:109
  136.8 55.8 %all-gather.7.cloned.1.call-done = bf16[1,2,1024,512]{3,2,1,0:T(8,128)(2,1)} async-done(((bf16[1,2,64,512]{3,2,1,0:T(8,128)(2,1)}), bf16[1,2,1024,512]{3,2,1,0:T(8,128)(2,1)}) %all-gather.7.cloned.1.call-update) | async-done | bytes 2097168 | tf_op jit(solution)/shard_map/all_gather | solution.py:78
  192.5 69.3 %all-gather.5.cloned.1.call-done = bf16[1,1024,1536]{2,1,0:T(8,128)(2,1)} async-done(((bf16[1,64,1536]{2,1,0:T(8,128)(2,1)}), bf16[1,1024,1536]{2,1,0:T(8,128)(2,1)}) %all-gather.5.cloned.1.call-update) | async-done | bytes 3145744 | tf_op jit(solution)/shard_map/all_gather | solution.py:76
  261.8 1.1 broadcast.171
  262.9 47.7 %while.13 = (s32[]{:T(128)}, bf16[3,2,80,1024]{3,2,1,0:T(8,128)(2,1)}, s32[]{:T(128)}, bf16[3,2,80,1024]{3,2,1,0:T(8,128)(2,1)}, f32[1,1024]{1,0:T(1,128)S(1)}, ...) while((s32[]{:T(128)}, ...), condition=%wide.region_10.11_spmd, body=%wide.region_0.10_spmd.sunk | while | flops 2827160064 | bytes 100394192 | solution.py:109
  262.9 1.3 collective-permute-start
  264.2 2.3 collective-permute-done
  266.5 39.3 %conditional.2 = (bf16[3,2,80,1024]{3,2,1,0:T(8,128)(2,1)}) conditional(s32[]{:T(128)} %convert_element_type.51, () %tuple.55, (s32[]{:T(128)}, bf16[3,2,80,1024]{3,2,1,0:T(8,128)(2,1)}, bf16[3,2,80,1024]{3,2,1,0:T(8,128)(2,1)S(1)}, f32[1,1024]{1,0:T(1,128)S(1)}, bf16[1,1024,1536]{2,1,0:T(8,128)(2,1)}, /*index=5*/bf16[1,2,1024,512]{3,2,1,0:T(8,128)(2,1)}, ...), branch_computations={%region_1.1_spmd, %region_2.9_spmd} | conditional | flops 2827160064 | bytes 96461808 | solution.py:107
  266.5 0.9 copy-done.7
  267.5 1.3 select_convert_fusion
  268.8 0.1 slice_reduce_fusion.1
  269.0 0.2 fusion.34
  269.2 0.2 slice_reduce_fusion
  269.4 0.2 multiply_convert_fusion.3
  269.6 0.3 multiply_reduce_fusion.1
  269.9 0.3 multiply_convert_fusion.1
  270.3 1.2 copy-done.10
  271.5 2.9 fusion.83
  274.4 0.5 fusion.25
  274.9 1.2 slice.90
  276.0 1.1 fusion.82
  277.2 1.9 fusion.81
  279.1 0.9 squeeze.39
  280.0 0.9 squeeze.40
  281.0 0.2 squeeze.38
  281.2 2.2 slice.87
  283.4 2.2 slice.85
  285.6 2.9 convolution_bitcast_fusion.1
  288.5 2.3 fusion.84
  290.8 1.3 broadcast_multiply_fusion
  292.2 0.2 copy-done.1
  292.3 0.2 copy-done.4
  292.5 1.4 multiply_reduce_fusion
  293.9 0.4 convolution_bitcast_fusion.3
  294.3 0.7 copy-done.3
  295.0 1.2 fusion.17
  296.2 1.0 convolution_convert_fusion
  297.2 2.2 copy.61
  299.4 2.2 concatenate.26
  301.7 0.1 copy.62
  301.8 2.1 fusion.28
  304.0 0.5 fusion.11
  304.6 1.3 fusion.7
  305.9 1.3 collective-permute-start
  307.2 2.3 collective-permute-done
  309.5 1.1 conditional.2
  309.5 1.1 broadcast.159
  310.6 2.1 copy.67
  312.7 41.8 %psum.7 = bf16[3,2,1024]{2,0,1:T(4,128)(2,1)S(1)} all-reduce(bf16[3,2,1024]{2,0,1:T(4,128)(2,1)S(1)} %fusion.71), channel_id=1, replica_groups=mesh['section'=2,'dp'=16] {'section'}, use_global_device_ids=true, to_apply=%region_11.12 | all-reduce | flops 6144 | bytes 24576 | tf_op jit(solution)/shard_map/psum | solution.py:21
  354.5 0.1 slice_reduce_fusion.3
  354.6 0.1 slice_reduce_fusion.2
  354.7 0.2 fusion.77
  355.1 0.2 multiply_reduce_fusion.2
  355.4 0.4 fusion.69
  355.8 0.6 slice_bitcast_fusion
  356.4 0.6 broadcast_in_dim.7
  (38 shorter events, 0.6 us)
Async XLA Ops:
  7.2 348.2 %copy-start = (bf16[1024,500]{0,1:T(8,128)(2,1)S(1)}, bf16[1024,500]{0,1:T(8,128)(2,1)}, u32[]{:S(2)}) copy-start(bf16[1024,500]{0,1:T(8,128)(2,1)} %param.19) | copy-start | bytes 3072004
  7.2 61.4 %all-gather.9.cloned.1.call-start = ((), (), s32[]{:S(2)}) async-start(), calls=%async_computation.2 | async-start | bytes 1114112 | tf_op jit(solution)/shard_map/all_gather | solution.py:77
  7.9 122.7 %all-gather.11.cloned.1.call-start = ((), (), s32[]{:S(2)}) async-start(), calls=%async_computation.3 | async-start | bytes 2228224 | tf_op jit(solution)/shard_map/all_gather | solution.py:79
  9.7 182.8 %all-gather.7.cloned.1.call-start = ((), (), s32[]{:S(2)}) async-start(), calls=%async_computation.1 | async-start | bytes 2228224 | tf_op jit(solution)/shard_map/all_gather | solution.py:78
  10.4 251.4 %all-gather.5.cloned.1.call-start = ((), (), s32[]{:S(2)}) async-start(), calls=%async_computation | async-start | bytes 3342336 | tf_op jit(solution)/shard_map/all_gather | solution.py:76
  70.9 192.0 %copy-start.8 = (f32[1,1024]{1,0:T(1,128)S(1)}, f32[1,1024]{1,0:T(1,128)}, u32[]{:S(2)}) copy-start(f32[1,1024]{1,0:T(1,128)} %param.17) | copy-start | bytes 12292
  262.9 3.7 %collective-permute-start = (bf16[3,2,80,1024]{3,2,1,0:T(8,128)(2,1)}, bf16[3,2,80,1024]{3,2,1,0:T(8,128)(2,1)S(1)}, u32[]{:S(2)}, u32[]{:S(2)}) collective-permute-start(bf16[3,2,80,1024]{3,2,1,0:T(8,128)(2,1)} %get-tuple-element.322), channel_id=1, source_target_pairs={{0,16},{1,17},{2,18},{3,19},{4,20},{5,21},{6,22},{7,23},{8,24},{9,... | collective-permute-start | bytes 2949128 | tf_op jit(solution)/shard_map/while/body/eval_jaxpr/ppermute | solution.py:16
  266.5 0.9 copy-start.7
  269.6 1.9 copy-start.10
  271.5 2.9 copy-start.6
  290.8 1.5 copy-start.1
  290.8 1.7 copy-start.4
  293.9 1.1 copy-start.3
  297.2 4.5 %copy-start.5 = (bf16[2,8,64,80]{3,2,1,0:T(8,128)(2,1)S(1)}, bf16[2,8,64,80]{3,2,1,0:T(8,128)(2,1)}, u32[]{:S(2)}) copy-start(bf16[2,8,64,80]{3,2,1,0:T(8,128)(2,1)} %convolution_convert_fusion) | copy-start | bytes 491524 | tf_op jit(solution)/shard_map/while/body/eval_jaxpr/cond
  301.8 2.2 copy-start.2
  305.9 3.7 %collective-permute-start = (bf16[3,2,80,1024]{3,2,1,0:T(8,128)(2,1)}, bf16[3,2,80,1024]{3,2,1,0:T(8,128)(2,1)S(1)}, u32[]{:S(2)}, u32[]{:S(2)}) collective-permute-start(bf16[3,2,80,1024]{3,2,1,0:T(8,128)(2,1)} %get-tuple-element.322), channel_id=1, source_target_pairs={{0,16},{1,17},{2,18},{3,19},{4,20},{5,21},{6,22},{7,23},{8,24},{9,... | collective-permute-start | bytes 2949128 | tf_op jit(solution)/shard_map/while/body/eval_jaxpr/ppermute | solution.py:16
  310.6 44.4 %copy-start.9 = (f32[1024]{0:T(1024)S(1)}, f32[1024]{0:T(1024)}, u32[]{:S(2)}) copy-start(f32[1024]{0:T(1024)} %param.18) | copy-start | bytes 12292
Sparse Core Ops, SparseCore 0:
  10.7 57.7 all-gather.8
  71.4 59.2 all-gather.10
  133.4 59.1 all-gather.6
  195.2 66.5 all-gather.4
where the time goes:
time: 364 us
  waiting for transfers between devices  247 us (68%)
  blocking collectives  41.8 us (11%)
  local copies, waits for them, and re-layouts  36.2 us (10%)
  matrix products  15.6 us (4%)
  between operations  13.8 us (4%)
  other arithmetic  6.18 us (2%)
    all_gather x1, waiting for transfers between devices, shards(): lax.all_gather(w_qkv, 'dp', axis=1, tiled=True)  69.3 us
    all_gather x1, waiting for transfers between devices, shards(): lax.all_gather(tangent_output, 'dp', axis=3, tiled=True)  59.7 us
    all_gather x1, waiting for transfers between devices, shards(): lax.all_gather(tangent_value, 'dp', axis=2, tiled=True)  55.8 us
    all_gather x1, waiting for transfers between devices, shards(): lax.all_gather(w_output, 'dp', axis=2, tiled=True)  55.5 us
    psum x1, blocking collectives, spread(): return lax.psum(jnp.where(mine, shard, jnp.zeros_like(shard)), axis)  41.8 us
    dot_general x10, matrix products, contract(): return jnp.einsum(spec, left, right, preferred_element_type=jnp.float32)  13.3 us
    while x3, local copies, waits for them, and re-layouts, shards(): lax.fori_loop(0, section_count, advance, jnp.zeros_like(entering))  10.5 us
  transfers between devices with their start and end apart: 6, of which 6 were waited for; matrix products, arithmetic and copies ran while one was open for 3% of the time, Pallas kernels for 0%

commit v1 on v0

--- a/solution.py
+++ b/solution.py
@@ -76,7 +76,7 @@
         lax.all_gather(w_qkv, "dp", axis=1, tiled=True),
         lax.all_gather(w_output, "dp", axis=2, tiled=True),
         lax.all_gather(tangent_value, "dp", axis=2, tiled=True),
-        lax.all_gather(tangent_output, "dp", axis=3, tiled=True),
+        jnp.concatenate(lax.all_gather(tangent_output, "dp"), axis=3),
     )
     section_gain = layer_gain[0]
 

time: 364 us -> 366 us (level)
  waiting for transfers between devices: 247 us -> 255 us
  local copies, waits for them, and re-layouts: 36.2 us -> 28.7 us
    while x3 -> x2, local copies, waits for them, and re-layouts: 10.5 us -> 4.34 us  [shards(): lax.fori_loop(0, section_count, advance, jnp.zeros_like(entering))]
    all_gather x1, waiting for transfers between devices: 55.8 us -> 59.7 us  [shards(): lax.all_gather(tangent_value, 'dp', axis=2, tiled=True)]
  transfers between devices with their start and end apart: 6 -> 6, of which waited for: 6 -> 6; matrix products, arithmetic and copies ran while one was open for 3% -> 1% of each run, Pallas kernels for 0% -> 0%
where the time goes in v1:
time: 366 us; the launch traced here: 365 us
  waiting for transfers between devices  255 us (70%)
  blocking collectives  42.4 us (12%)
  local copies, waits for them, and re-layouts  28.7 us (8%)
  matrix products  16 us (4%)
  between operations  13.8 us (4%)
  other arithmetic  6.28 us (2%)
    all_gather x1, waiting for transfers between devices, shards(): lax.all_gather(w_qkv, 'dp', axis=1, tiled=True)  69.3 us
    all_gather x1, waiting for transfers between devices, shards(): lax.all_gather(tangent_output, 'dp')  61.9 us
    all_gather x1, waiting for transfers between devices, shards(): lax.all_gather(tangent_value, 'dp', axis=2, tiled=True)  59.7 us
    all_gather x1, waiting for transfers between devices, shards(): lax.all_gather(w_output, 'dp', axis=2, tiled=True)  56.6 us
    psum x1, blocking collectives, spread(): return lax.psum(jnp.where(mine, shard, jnp.zeros_like(shard)), axis)  42.4 us
    dot_general x10, matrix products, contract(): return jnp.einsum(spec, left, right, preferred_element_type=jnp.float32)  13.7 us
  transfers between devices with their start and end apart: 6, of which 6 were waited for; matrix products, arithmetic and copies ran while one was open for 1% of the time, Pallas kernels for 0%

profile of v1, /device:TPU:0, one launch (start us, length us, event | category | flops | bytes accessed | tf_op | source)
XLA Modules:
  0.0 364.9 jit_solution(17337097851367675491)
XLA Ops:
  7.2 0.7 all-gather.10.cloned.1.call-update
  8.0 0.7 all-gather.8.cloned.1.call-update
  8.7 0.7 all-gather.12.cloned.1.call-update
  9.4 0.5 all-gather.6.cloned.1.call-update
  10.0 2.0 concatenate.31
  12.0 56.6 %all-gather.10.cloned.1.call-done = bf16[1,512,1024]{1,2,0:T(8,128)(2,1)} async-done(((bf16[1,512,64]{1,2,0:T(8,128)(2,1)}), bf16[1,512,1024]{1,2,0:T(8,128)(2,1)}) %all-gather.10.cloned.1.call-update) | async-done | bytes 1048592 | tf_op jit(solution)/shard_map/all_gather | solution.py:77
  68.6 2.3 copy.67
  70.9 59.7 %all-gather.8.cloned.1.call-done = bf16[1,2,1024,512]{3,2,1,0:T(8,128)(2,1)} async-done(((bf16[1,2,64,512]{3,2,1,0:T(8,128)(2,1)}), bf16[1,2,1024,512]{3,2,1,0:T(8,128)(2,1)}) %all-gather.8.cloned.1.call-update) | async-done | bytes 2097168 | tf_op jit(solution)/shard_map/all_gather | solution.py:78
  130.5 61.9 %all-gather.12.cloned.1.call-done = bf16[16,2,512,64]{2,3,0,1:T(8,128)(2,1)} async-done(((bf16[1,2,512,64]{2,3,0,1:T(8,128)(2,1)}), bf16[16,2,512,64]{2,3,0,1:T(8,128)(2,1)}) %all-gather.12.cloned.1.call-update) | async-done | bytes 2097168 | tf_op jit(solution)/shard_map/all_gather | solution.py:79
  192.4 69.3 %all-gather.6.cloned.1.call-done = bf16[1,1024,1536]{2,1,0:T(8,128)(2,1)} async-done(((bf16[1,64,1536]{2,1,0:T(8,128)(2,1)}), bf16[1,1024,1536]{2,1,0:T(8,128)(2,1)}) %all-gather.6.cloned.1.call-update) | async-done | bytes 3145744 | tf_op jit(solution)/shard_map/all_gather | solution.py:76
  261.7 1.2 broadcast.171
  262.8 48.5 %while.13 = (s32[]{:T(128)}, bf16[3,2,80,1024]{3,2,1,0:T(8,128)(2,1)}, s32[]{:T(128)}, bf16[3,2,80,1024]{3,2,1,0:T(8,128)(2,1)}, f32[1,1024]{1,0:T(1,128)S(1)}, ...) while((s32[]{:T(128)}, ...), condition=%wide.region_10.11_spmd, body=%wide.region_0.10_spmd.sunk | while | flops 2827160064 | bytes 100394192 | solution.py:109
  262.8 1.3 collective-permute-start
  264.2 2.3 collective-permute-done
  266.5 40.0 %conditional.2 = (bf16[3,2,80,1024]{3,2,1,0:T(8,128)(2,1)}) conditional(s32[]{:T(128)} %convert_element_type.51, () %tuple.55, (s32[]{:T(128)}, bf16[3,2,80,1024]{3,2,1,0:T(8,128)(2,1)}, bf16[3,2,80,1024]{3,2,1,0:T(8,128)(2,1)S(1)}, f32[1,1024]{1,0:T(1,128)S(1)}, bf16[1,1024,1536]{2,1,0:T(8,128)(2,1)}, /*index=5*/bf16[1,2,1024,512]{3,2,1,0:T(8,128)(2,1)}, ...), branch_computations={%region_1.1_spmd, %region_2.9_spmd} | conditional | flops 2827160064 | bytes 96461808 | solution.py:107
  266.5 1.0 copy-done.7
  267.6 1.3 select_convert_fusion
  268.9 0.1 slice_reduce_fusion.1
  269.0 0.2 fusion.27
  269.3 0.2 slice_reduce_fusion
  269.4 0.2 multiply_convert_fusion.3
  269.6 0.3 multiply_reduce_fusion.1
  270.0 0.3 multiply_convert_fusion.1
  270.3 1.2 copy-done.10
  271.5 2.9 fusion.76
  274.4 0.5 fusion.18
  275.0 1.2 slice.90
  276.2 1.1 fusion.75
  277.3 1.9 fusion.74
  279.2 1.0 squeeze.36
  280.2 0.9 squeeze.37
  281.2 0.2 squeeze.35
  281.3 2.2 slice.87
  283.6 2.2 slice.85
  285.8 2.9 convolution_bitcast_fusion.2
  288.7 2.3 fusion.77
  291.0 1.3 broadcast_multiply_fusion
  292.4 0.2 copy-done.1
  292.5 0.2 copy-done.3
  292.7 1.4 multiply_reduce_fusion
  294.1 0.4 convolution_bitcast_fusion.4
  294.5 0.7 copy-done.2
  295.2 1.2 fusion.10
  296.4 1.0 convolution_convert_fusion
  297.4 2.3 copy.62
  299.7 2.2 concatenate.26
  301.9 0.1 copy.63
  302.1 2.1 fusion.21
  304.2 0.9 fusion.6
  305.2 1.4 fusion.5
  306.5 1.3 collective-permute-start
  307.9 2.3 collective-permute-done
  310.2 1.2 conditional.2
  310.2 1.2 broadcast.159
  311.4 2.1 copy.68
  313.5 42.4 %psum.7 = bf16[3,2,1024]{2,0,1:T(4,128)(2,1)S(1)} all-reduce(bf16[3,2,1024]{2,0,1:T(4,128)(2,1)S(1)} %fusion.64), channel_id=1, replica_groups=mesh['section'=2,'dp'=16] {'section'}, use_global_device_ids=true, to_apply=%region_11.12 | all-reduce | flops 6144 | bytes 24576 | tf_op jit(solution)/shard_map/psum | solution.py:21
  355.9 0.1 slice_reduce_fusion.3
  356.0 0.1 slice_reduce_fusion.2
  356.1 0.2 fusion.70
  356.4 0.2 multiply_reduce_fusion.2
  356.7 0.1 multiply_convert_fusion.4
  356.8 0.4 fusion.62
  357.2 0.6 slice_bitcast_fusion
  357.8 0.6 broadcast_in_dim.7
  (36 shorter events, 0.5 us)
Async XLA Ops:
  7.2 349.6 %copy-start = (bf16[1024,500]{0,1:T(8,128)(2,1)S(1)}, bf16[1024,500]{0,1:T(8,128)(2,1)}, u32[]{:S(2)}) copy-start(bf16[1024,500]{0,1:T(8,128)(2,1)} %param.19) | copy-start | bytes 3072004
  7.2 61.4 %all-gather.10.cloned.1.call-start = ((), (), s32[]{:S(2)}) async-start(), calls=%async_computation.2 | async-start | bytes 1114112 | tf_op jit(solution)/shard_map/all_gather | solution.py:77
  7.9 122.6 %all-gather.8.cloned.1.call-start = ((), (), s32[]{:S(2)}) async-start(), calls=%async_computation.1 | async-start | bytes 2228224 | tf_op jit(solution)/shard_map/all_gather | solution.py:78
  8.7 183.8 %all-gather.12.cloned.1.call-start = ((), (), s32[]{:S(2)}) async-start(), calls=%async_computation.3 | async-start | bytes 2228224 | tf_op jit(solution)/shard_map/all_gather | solution.py:79
  9.4 252.3 %all-gather.6.cloned.1.call-start = ((), (), s32[]{:S(2)}) async-start(), calls=%async_computation | async-start | bytes 3342336 | tf_op jit(solution)/shard_map/all_gather | solution.py:76
  12.0 250.8 %copy-start.8 = (f32[1,1024]{1,0:T(1,128)S(1)}, f32[1,1024]{1,0:T(1,128)}, u32[]{:S(2)}) copy-start(f32[1,1024]{1,0:T(1,128)} %param.17) | copy-start | bytes 12292
  262.8 3.7 %collective-permute-start = (bf16[3,2,80,1024]{3,2,1,0:T(8,128)(2,1)}, bf16[3,2,80,1024]{3,2,1,0:T(8,128)(2,1)S(1)}, u32[]{:S(2)}, u32[]{:S(2)}) collective-permute-start(bf16[3,2,80,1024]{3,2,1,0:T(8,128)(2,1)} %get-tuple-element.322), channel_id=1, source_target_pairs={{0,16},{1,17},{2,18},{3,19},{4,20},{5,21},{6,22},{7,23},{8,24},{9,... | collective-permute-start | bytes 2949128 | tf_op jit(solution)/shard_map/while/body/eval_jaxpr/ppermute | solution.py:16
  266.5 1.0 copy-start.7
  269.6 1.9 copy-start.10
  271.5 2.9 copy-start.6
  291.0 1.5 copy-start.1
  291.0 1.7 copy-start.3
  294.1 1.1 copy-start.2
  297.4 4.6 %copy-start.4 = (bf16[2,8,64,80]{3,2,1,0:T(8,128)(2,1)S(1)}, bf16[2,8,64,80]{3,2,1,0:T(8,128)(2,1)}, u32[]{:S(2)}) copy-start(bf16[2,8,64,80]{3,2,1,0:T(8,128)(2,1)} %convolution_convert_fusion) | copy-start | bytes 491524 | tf_op jit(solution)/shard_map/while/body/eval_jaxpr/cond
  302.1 2.2 copy-start.5
  306.5 3.7 %collective-permute-start = (bf16[3,2,80,1024]{3,2,1,0:T(8,128)(2,1)}, bf16[3,2,80,1024]{3,2,1,0:T(8,128)(2,1)S(1)}, u32[]{:S(2)}, u32[]{:S(2)}) collective-permute-start(bf16[3,2,80,1024]{3,2,1,0:T(8,128)(2,1)} %get-tuple-element.322), channel_id=1, source_target_pairs={{0,16},{1,17},{2,18},{3,19},{4,20},{5,21},{6,22},{7,23},{8,24},{9,... | collective-permute-start | bytes 2949128 | tf_op jit(solution)/shard_map/while/body/eval_jaxpr/ppermute | solution.py:16
  311.4 45.0 %copy-start.9 = (f32[1024]{0:T(1024)S(1)}, f32[1024]{0:T(1024)}, u32[]{:S(2)}) copy-start(f32[1024]{0:T(1024)} %param.18) | copy-start | bytes 12292
Sparse Core Ops, SparseCore 0:
  10.7 57.7 all-gather.9
  71.3 59.1 all-gather.7
  133.3 59.0 all-gather.11
  195.0 66.5 all-gather.5
